TPU v7x, 32 devices: a whole 2x2x4 slice. The times are simulated.
32 devices in a mesh: band: 8 (over z, x), slab: 4 (over y, core).
Axes of the slice: x: 2, y: 2, z: 4, core: 2. Of those that a mesh axis runs over, the one named last changes fastest.
Arguments:
- orbitals: float32 [512, 64, 512], P('band', 'slab'), may hold values from -6 to 6
- potential: float32 [64, 512], P('slab'), may hold values from 0 to 1
- projectors: float32 [4, 2048, 128], replicated, may hold values from -0.125 to 0.125
- atom_kind: int32 [32], P('slab'), may hold values from 0 to 3
- atom_plane: int32 [32], P('slab'), may hold values from 0 to 60, as said below
- atom_coef: float32 [32, 128], P('slab'), may hold values from 0.2 to 1
- filter_cut: float32 [1], replicated, may hold values from 0.5 to 2
- filter_top: float32 [1], replicated, may hold values from 9 to 14
Outputs:
- new_orbitals: float32 [512, 32768], P(None, ('slab', 'band'))
Inputs may be any that keep to these rules, and one draw needn't show every extreme that they name: `atom_plane`: block i's 4 planes lie inside the slab of planes (i // 8) * 16 to (i // 8 + 1) * 16 - 1; blocks may share planes.
All inputs are finite; a program needn't handle non-finite values.
Results may differ from a plain program's by a relative error of at most 0.0003.
Values sent between devices are 32-bit elements; how exact they have to be, the bound alone decides.
A program may use at most 128 MiB of HBM per device.

v0:
```python
import jax
import jax.numpy as jnp
from jax import lax
from jax.sharding import PartitionSpec as P

GZ = 32
ORDER = 6


low_edge = -1.0
near_coef = 4.0 / 3.0
far_coef = -1.0 / 12.0
self_coef = -2.5
highest = lax.Precision.HIGHEST


def padded_2(value, sides, width):
    for axis, dim in sides:
        size, length = (lax.axis_size(axis), value.shape[dim])
        up = [(i, (i + 1) % size) for i in range(size)]
        down = [(j, i) for i, j in up]
        last = lax.slice_in_dim(value, length - width, length, axis=dim)
        first = lax.slice_in_dim(value, 0, width, axis=dim)
        before = lax.ppermute(last, axis, up)
        after = lax.ppermute(first, axis, down)
        value = jnp.concatenate([before, value, after], axis=dim)
    return value


def shifted(source, offset):
    if offset > 0:
        zeros_part = jnp.zeros(source.shape[:-1] + (offset,), source.dtype)
        return jnp.concatenate([zeros_part, source[..., :-offset]], axis=-1)
    zeros_part = jnp.zeros(source.shape[:-1] + (-offset,), source.dtype)
    return jnp.concatenate([source[..., -offset:], zeros_part], axis=-1)


def transverse(source, width_z):
    length_last = source.shape[-1]
    z_position = jnp.arange(length_last) % width_z
    result_sum = 2.0 * self_coef * source
    for offset, weight_coef in ((1, near_coef), (-1, near_coef), (2, far_coef), (-2, far_coef)):
        result_sum = result_sum + weight_coef * shifted(source, offset * width_z)
        inside = (z_position - offset >= 0) & (z_position - offset < width_z)
        result_sum = result_sum + weight_coef * jnp.where(inside, shifted(source, offset), 0.0)
    return result_sum


def local(
    orbitals, potential, projectors, atom_kind, atom_plane, atom_coef, filter_cut, filter_top
):
    band_count, planes, points = orbitals.shape
    kind_count, block_pts, func_count = projectors.shape
    atom_count = atom_kind.shape[0]
    block_depth = block_pts // points
    local_plane = atom_plane - lax.axis_index("slab") * planes
    plane_ids = jnp.arange(planes)
    depth_ids = jnp.arange(block_depth)
    selector = (
        plane_ids[None, None, :] == local_plane[:, None, None] + depth_ids[None, :, None]
    ).astype(jnp.float32)
    atom_tables = jnp.take(projectors, atom_kind, axis=0)
    coef_rows = atom_coef[:, None, :]

    def hamiltonian_fn(source):
        padded = padded_2(source, (("slab", 1),), 2)
        along_x = self_coef * source
        along_x = along_x + near_coef * (padded[:, 1 : planes + 1] + padded[:, 3 : planes + 3])
        along_x = along_x + far_coef * (padded[:, 0:planes] + padded[:, 4 : planes + 4])
        laplace = along_x + transverse(source, GZ)
        blocks = jnp.einsum("ajx,nxp->anjp", selector, source, precision=highest)
        blocks = blocks.reshape(atom_count, band_count, block_pts)
        coupled = jnp.einsum("anq,aqf->anf", blocks, atom_tables, precision=highest) * coef_rows
        spread_back = jnp.einsum("anf,aqf->anq", coupled, atom_tables, precision=highest)
        spread_back = spread_back.reshape(atom_count, band_count, block_depth, points)
        nonlocal_part = jnp.einsum("ajx,anjp->nxp", selector, spread_back, precision=highest)
        return -0.5 * laplace + potential[None] * source + nonlocal_part

    cut_value = filter_cut[0]
    top_value = filter_top[0]
    half_width = (top_value - cut_value) / 2.0
    centre = (top_value + cut_value) / 2.0
    sigma_now = half_width / (low_edge - centre)
    tau_value = 2.0 / sigma_now
    previous = orbitals
    current = (hamiltonian_fn(previous) - centre * previous) * (sigma_now / half_width)
    for step_index in range(ORDER - 1):
        sigma_next = 1.0 / (tau_value - sigma_now)
        upcoming = (hamiltonian_fn(current) - centre * current) * (
            2.0 * sigma_next / half_width
        ) - sigma_now * sigma_next * previous
        previous = current
        current = upcoming
        sigma_now = sigma_next
    flat_orbitals = current.reshape(band_count, planes * points)
    grid_layout = lax.all_to_all(flat_orbitals, "band", split_axis=1, concat_axis=0, tiled=True)
    point_total = grid_layout.shape[1] * lax.axis_size(("band", "slab"))
    partial_gram = jnp.dot(grid_layout, grid_layout.T, precision=highest) / point_total
    gram_matrix = lax.psum(partial_gram, ("band", "slab"))
    factor = jnp.linalg.cholesky(gram_matrix)
    return jax.scipy.linalg.solve_triangular(factor, grid_layout, lower=True)


def solution(mesh):
    in_specs = (
        P("band", "slab", None),
        P("slab", None),
        P(),
        P("slab"),
        P("slab"),
        P("slab", None),
        P(),
        P(),
    )
    out_specs = P(None, ("slab", "band"))
    return jax.shard_map(local, mesh=mesh, in_specs=in_specs, out_specs=out_specs, check_vma=False)
```

profile of v0, /device:TPU:0, one launch (start us, length us, event | category | flops | bytes accessed | tf_op | source)
XLA Modules:
  0.0 782.5 jit_solution(11253992471097181108)
XLA Ops:
  31.2 6.9 copy.17
  38.1 6.3 reshape.122
  44.4 6.6 gather_fusion
  51.0 10.4 %convolution_multiply_fusion.6 = f32[8,64,128]{2,1,0:T(8,128)S(1)} fusion(f32[8,64,2048]{2,1,0:T(8,128)} %reshape.122, f32[8,128]{1,0:T(8,128)S(1)} %copy-done.24, f32[8,2048,128]{2,1,0:T(8,128)} %gather_fusion, pred[8]{0:T(512)(128)(4,1)S(1)} %compare_and_fusion), kind=kOutput, calls=%fused_computation.154 | convolution fusion | flops 1612775424 | bytes 12849160 | tf_op jit(solution)/shard_map/anq,aqf->anf/dot_general | solution.py:73
  61.5 10.5 %fusion.153 = f32[8,64,2048]{2,1,0:T(8,128)} fusion(f32[8,64,128]{2,1,0:T(8,128)S(1)} %convolution_multiply_fusion.6, f32[8,2048,128]{2,1,0:T(8,128)S(1)} %copy-done, pred[8]{0:T(512)(128)(4,1)S(1)} %compare_and_fusion), kind=kOutput, calls=%fused_computation.243 | convolution fusion | flops 1612709888 | bytes 12845064 | tf_op jit(solution)/shard_map/anf,aqf->anq/dot_general | solution.py:74
  81.7 12.0 %fusion.75 = f32[64,16,512]{2,1,0:T(8,128)S(1)} fusion(f32[64,2,512]{2,1,0:T(2,128)S(1)} %collective-permute-done, f32[64,16,512]{2,1,0:T(8,128)S(1)} %copy-done.1, f32[64,18,512]{2,1,0:T(8,128)} %copy-done.23, f32[64,16,510]{2,1,0:T(8,128)} %get-tuple-element.84, f32[64,16,448]{2,1,0:T(8,128)} %get-tuple-element.82, ...), kind=kOutput, calls=%fused_computation.107 | convolution fusion | flops 221249536 | bytes 28846600 | tf_op jit(solution)/shard_map/ajx,anjp->nxp/dot_general | solution.py:76
  115.4 9.3 %convolution_multiply_fusion.5 = f32[8,64,128]{2,1,0:T(8,128)S(1)} fusion(f32[8,64,2048]{2,1,0:T(8,128)} %reshape.124, f32[8,128]{1,0:T(8,128)S(1)} %copy-done.24, f32[8,2048,128]{2,1,0:T(8,128)} %gather_fusion, pred[8]{0:T(512)(128)(4,1)S(1)} %compare_and_fusion), kind=kOutput, calls=%fused_computation.153 | convolution fusion | flops 1612775424 | bytes 12849160 | tf_op jit(solution)/shard_map/anq,aqf->anf/dot_general | solution.py:73
  124.7 12.7 %fusion.152 = f32[8,64,2048]{2,1,0:T(8,128)} fusion(f32[8,64,128]{2,1,0:T(8,128)S(1)} %convolution_multiply_fusion.5, f32[8,2048,128]{2,1,0:T(8,128)} %gather_fusion, pred[8]{0:T(512)(128)(4,1)S(1)} %compare_and_fusion), kind=kOutput, calls=%fused_computation.242 | convolution fusion | flops 1612709888 | bytes 12845064 | tf_op jit(solution)/shard_map/anf,aqf->anq/dot_general | solution.py:74
  150.8 12.0 %fusion.63 = f32[64,16,512]{2,1,0:T(8,128)S(1)} fusion(f32[64,16,512]{2,1,0:T(8,128)S(1)} %copy-done.9, f32[64,2,512]{2,1,0:T(2,128)S(1)} %collective-permute-done.3, f32[64,2,512]{2,1,0:T(2,128)S(1)} %collective-permute-done.2, f32[64,16,512]{2,1,0:T(8,128)S(1)} %copy-done.1, f32[64,16,510]{2,1,0:T(8,128)} %get-tuple-element.74, ...), kind=kOutput, calls=%fused_computation.95 | convolution fusion | flops 223346688 | bytes 27011596 | tf_op jit(solution)/shard_map/ajx,anjp->nxp/dot_general | solution.py:76
  184.6 9.1 %convolution_multiply_fusion.4 = f32[8,64,128]{2,1,0:T(8,128)S(1)} fusion(f32[8,64,2048]{2,1,0:T(8,128)} %reshape.126, f32[8,128]{1,0:T(8,128)S(1)} %copy-done.24, f32[8,2048,128]{2,1,0:T(8,128)} %gather_fusion, pred[8]{0:T(512)(128)(4,1)S(1)} %compare_and_fusion), kind=kOutput, calls=%fused_computation.152 | convolution fusion | flops 1612775424 | bytes 12849160 | tf_op jit(solution)/shard_map/anq,aqf->anf/dot_general | solution.py:73
  193.7 12.7 %fusion.151 = f32[8,64,2048]{2,1,0:T(8,128)} fusion(f32[8,64,128]{2,1,0:T(8,128)S(1)} %convolution_multiply_fusion.4, f32[8,2048,128]{2,1,0:T(8,128)} %gather_fusion, pred[8]{0:T(512)(128)(4,1)S(1)} %compare_and_fusion), kind=kOutput, calls=%fused_computation.241 | convolution fusion | flops 1612709888 | bytes 12845064 | tf_op jit(solution)/shard_map/anf,aqf->anq/dot_general | solution.py:74
  220.0 12.3 %fusion.50 = f32[64,16,512]{2,1,0:T(8,128)S(1)} fusion(f32[64,16,512]{2,1,0:T(8,128)S(1)} %copy-done.6, f32[64,2,512]{2,1,0:T(2,128)S(1)} %collective-permute-done.5, f32[64,2,512]{2,1,0:T(2,128)S(1)} %collective-permute-done.4, f32[64,16,512]{2,1,0:T(8,128)S(1)} %copy-done.10, f32[64,16,510]{2,1,0:T(8,128)} %get-tuple-element.64, ...), kind=kOutput, calls=%fused_computation.82 | convolution fusion | flops 223346688 | bytes 27011596 | tf_op jit(solution)/shard_map/ajx,anjp->nxp/dot_general | solution.py:76
  254.0 9.0 %convolution_multiply_fusion.3 = f32[8,64,128]{2,1,0:T(8,128)S(1)} fusion(f32[8,64,2048]{2,1,0:T(8,128)} %reshape.128, f32[8,128]{1,0:T(8,128)S(1)} %copy-done.24, f32[8,2048,128]{2,1,0:T(8,128)} %gather_fusion, pred[8]{0:T(512)(128)(4,1)S(1)} %compare_and_fusion), kind=kOutput, calls=%fused_computation.151 | convolution fusion | flops 1612775424 | bytes 12849160 | tf_op jit(solution)/shard_map/anq,aqf->anf/dot_general | solution.py:73
  263.0 12.7 %fusion.150 = f32[8,64,2048]{2,1,0:T(8,128)} fusion(f32[8,64,128]{2,1,0:T(8,128)S(1)} %convolution_multiply_fusion.3, f32[8,2048,128]{2,1,0:T(8,128)} %gather_fusion, pred[8]{0:T(512)(128)(4,1)S(1)} %compare_and_fusion), kind=kOutput, calls=%fused_computation.240 | convolution fusion | flops 1612709888 | bytes 12845064 | tf_op jit(solution)/shard_map/anf,aqf->anq/dot_general | solution.py:74
  289.2 13.8 %fusion.37 = f32[64,16,512]{2,1,0:T(8,128)S(1)} fusion(f32[64,16,512]{2,1,0:T(8,128)} %copy-done.2, f32[64,2,512]{2,1,0:T(2,128)S(1)} %collective-permute-done.7, f32[64,2,512]{2,1,0:T(2,128)S(1)} %collective-permute-done.6, f32[64,16,512]{2,1,0:T(8,128)S(1)} %copy-done.7, f32[64,16,510]{2,1,0:T(8,128)} %get-tuple-element.54, ...), kind=kOutput, calls=%fused_computation.69 | convolution fusion | flops 223346688 | bytes 27011596 | tf_op jit(solution)/shard_map/ajx,anjp->nxp/dot_general | solution.py:76
  324.6 9.3 %convolution_multiply_fusion.2 = f32[8,64,128]{2,1,0:T(8,128)S(1)} fusion(f32[8,64,2048]{2,1,0:T(8,128)} %reshape.130, f32[8,128]{1,0:T(8,128)S(1)} %copy-done.24, f32[8,2048,128]{2,1,0:T(8,128)} %gather_fusion, pred[8]{0:T(512)(128)(4,1)S(1)} %compare_and_fusion), kind=kOutput, calls=%fused_computation.150 | convolution fusion | flops 1612775424 | bytes 12849160 | tf_op jit(solution)/shard_map/anq,aqf->anf/dot_general | solution.py:73
  333.8 12.7 %fusion.149 = f32[8,64,2048]{2,1,0:T(8,128)} fusion(f32[8,64,128]{2,1,0:T(8,128)S(1)} %convolution_multiply_fusion.2, f32[8,2048,128]{2,1,0:T(8,128)} %gather_fusion, pred[8]{0:T(512)(128)(4,1)S(1)} %compare_and_fusion), kind=kOutput, calls=%fused_computation.239 | convolution fusion | flops 1612709888 | bytes 12845064 | tf_op jit(solution)/shard_map/anf,aqf->anq/dot_general | solution.py:74
  359.9 12.0 %fusion.24 = f32[64,16,512]{2,1,0:T(8,128)S(1)} fusion(f32[64,16,512]{2,1,0:T(8,128)S(1)} %fusion.37, f32[64,2,512]{2,1,0:T(2,128)S(1)} %collective-permute-done.9, f32[64,2,512]{2,1,0:T(2,128)S(1)} %collective-permute-done.8, f32[64,16,512]{2,1,0:T(8,128)S(1)} %copy-done.3, f32[64,16,510]{2,1,0:T(8,128)} %get-tuple-element.44, ...), kind=kOutput, calls=%fused_computation.56 | convolution fusion | flops 223346688 | bytes 27011596 | tf_op jit(solution)/shard_map/ajx,anjp->nxp/dot_general | solution.py:76
  393.5 9.3 %convolution_multiply_fusion.1 = f32[8,64,128]{2,1,0:T(8,128)S(1)} fusion(f32[8,64,2048]{2,1,0:T(8,128)} %reshape.132, f32[8,128]{1,0:T(8,128)S(1)} %copy-done.24, f32[8,2048,128]{2,1,0:T(8,128)} %gather_fusion, pred[8]{0:T(512)(128)(4,1)S(1)} %compare_and_fusion), kind=kOutput, calls=%fused_computation.149 | convolution fusion | flops 1612775424 | bytes 12849160 | tf_op jit(solution)/shard_map/anq,aqf->anf/dot_general | solution.py:73
  402.8 12.8 %fusion.148 = f32[8,64,2048]{2,1,0:T(8,128)} fusion(f32[8,64,128]{2,1,0:T(8,128)S(1)} %convolution_multiply_fusion.1, f32[8,2048,128]{2,1,0:T(8,128)} %gather_fusion, pred[8]{0:T(512)(128)(4,1)S(1)} %compare_and_fusion), kind=kOutput, calls=%fused_computation.238 | convolution fusion | flops 1612709888 | bytes 12845064 | tf_op jit(solution)/shard_map/anf,aqf->anq/dot_general | solution.py:74
  428.9 12.5 %fusion.11 = f32[64,16,512]{2,1,0:T(8,128)} fusion(f32[64,16,512]{2,1,0:T(8,128)S(1)} %copy-done.12, f32[64,2,512]{2,1,0:T(2,128)S(1)} %collective-permute-done.11, f32[64,2,512]{2,1,0:T(2,128)S(1)} %collective-permute-done.10, f32[64,16,512]{2,1,0:T(8,128)S(1)} %fusion.37, f32[64,16,510]{2,1,0:T(8,128)} %get-tuple-element.34, ...), kind=kOutput, calls=%fused_computation.43 | convolution fusion | flops 223346688 | bytes 27011596 | tf_op jit(solution)/shard_map/ajx,anjp->nxp/dot_general | solution.py:76
  444.5 55.2 %all_to_all.19 = f32[64,8,1024]{2,0,1:T(8,128)S(1)} all-to-all(f32[64,8,1024]{2,0,1:T(8,128)S(1)} %copy.29), channel_id=1, replica_groups=mesh['band'=8,'slab'=4] {'band'}, dimensions={1} | all-to-all | bytes 4194304 | tf_op jit(solution)/shard_map/all_to_all | solution.py:96
  505.5 128.1 %all-reduce.51.cloned.1.call-done = f32[512,512]{0,1:T(8,128)} async-done(((f32[512,512]{0,1:T(8,128)}), f32[512,512]{0,1:T(8,128)}) %all-reduce.51.cloned.1.call-update) | async-done | bytes 1048592 | tf_op jit(solution)/shard_map/psum | solution.py:99
  635.5 11.7 %cholesky.104 = f32[128,128]{1,0:T(8,128)S(1)} custom-call(f32[128,128]{1,0:T(8,128)S(1)} %cholesky.266), custom_call_target="Cholesky" | custom-call | tf_op jit(solution)/shard_map/jit(cholesky)/cholesky | solution.py:100
  647.4 9.8 %custom-call.31 = f32[1,128,128]{1,2,0:T(8,128)S(1)} custom-call(f32[1,128,128]{2,1,0:T(8,128)S(1)} %get-tuple-element.96), custom_call_target="InvertDiagBlocksLowerTriangular" | custom-call | tf_op jit(solution)/shard_map/jit(cholesky)/cholesky | solution.py:100
  657.9 11.9 %cholesky.217 = f32[128,128]{1,0:T(8,128)S(1)} custom-call(f32[128,128]{1,0:T(8,128)S(1)} %cholesky.270), custom_call_target="Cholesky" | custom-call | tf_op jit(solution)/shard_map/jit(cholesky)/cholesky | solution.py:100
  671.2 9.8 %custom-call.32 = f32[1,128,128]{1,2,0:T(8,128)S(1)} custom-call(f32[1,128,128]{2,1,0:T(8,128)S(1)} %get-tuple-element.93), custom_call_target="InvertDiagBlocksLowerTriangular" | custom-call | tf_op jit(solution)/shard_map/jit(cholesky)/cholesky | solution.py:100
  681.7 11.7 %cholesky.238 = f32[128,128]{1,0:T(8,128)S(1)} custom-call(f32[128,128]{1,0:T(8,128)S(1)} %cholesky.275), custom_call_target="Cholesky" | custom-call | tf_op jit(solution)/shard_map/jit(cholesky)/cholesky | solution.py:100
  694.1 9.8 %custom-call.33 = f32[1,128,128]{1,2,0:T(8,128)S(1)} custom-call(f32[1,128,128]{2,1,0:T(8,128)S(1)} %get-tuple-element.90), custom_call_target="InvertDiagBlocksLowerTriangular" | custom-call | tf_op jit(solution)/shard_map/jit(cholesky)/cholesky | solution.py:100
  704.5 11.9 %cholesky.255 = f32[128,128]{1,0:T(8,128)S(1)} custom-call(f32[128,128]{1,0:T(8,128)S(1)} %convolution_subtract_fusion.4), custom_call_target="Cholesky" | custom-call | tf_op jit(solution)/shard_map/jit(cholesky)/cholesky | solution.py:100
  719.9 8.4 %while.1 = (s32[]{:T(128)}, f32[512,512]{1,0:T(8,128)S(1)}, s32[4,2]{0,1:T(2,128)S(1)}, f32[4,128,128]{2,1,0:T(8,128)S(1)}, s32[]{:T(128)}) while((s32[]{:T(128)}, f32[512,512]{1,0:T(8,128)S(1)}, s32[4,2]{0,1:T(2,128)S(1)}, f32[4,128,128]{2,1,0:T(8,128)S(1)}, s32[]{:T(128)}) %tuple.61), condition=%wide.while_cond, body=%wide.while_body.sunk | while | flops 2 | bytes 131181 | solution.py:101
  728.3 39.3 %custom-call.34 = f32[4,128,128]{1,2,0:T(8,128)S(1)} custom-call(f32[4,128,128]{2,1,0:T(8,128)S(1)} %get-tuple-element.12), custom_call_target="InvertDiagBlocksLowerTriangular" | custom-call | tf_op jit(solution)/shard_map/jit(_solve_triangular)/triangular_solve | solution.py:101
  (188 shorter events, 239.3 us)
Async XLA Ops:
  6.5 627.1 %all-reduce.51.cloned.1.call-start = ((), (), s32[]{:S(2)}) async-start(), calls=%async_computation.1 | async-start | bytes 2097152 | tf_op jit(solution)/shard_map/psum | solution.py:99
  8.3 70.2 %collective-permute-start.1 = (f32[64,2,512]{2,1,0:T(2,128)S(1)}, f32[64,2,512]{2,1,0:T(2,128)S(1)}, u32[]{:S(2)}, u32[]{:S(2)}) collective-permute-start(f32[64,2,512]{2,1,0:T(2,128)S(1)} %get-tuple-element.85), channel_id=1, source_target_pairs={{1,0},{2,1},{3,2},{0,3},{5,4},{6,5},{7,6},{4,7},{9,8},{10,9},{11,1... | collective-permute-start | bytes 786440 | tf_op jit(solution)/shard_map/ppermute | solution.py:25
  10.8 67.9 %collective-permute-start = (f32[64,2,512]{2,1,0:T(2,128)S(1)}, f32[64,2,512]{2,1,0:T(2,128)S(1)}, u32[]{:S(2)}, u32[]{:S(2)}) collective-permute-start(f32[64,2,512]{2,1,0:T(2,128)S(1)} %get-tuple-element.86), channel_id=1, source_target_pairs={{0,1},{1,2},{2,3},{3,0},{4,5},{5,6},{6,7},{7,4},{8,9},{9,10},{10,1... | collective-permute-start | bytes 786440 | tf_op jit(solution)/shard_map/ppermute | solution.py:24
  44.4 6.6 copy-start.24
  51.0 10.4 %copy-start = (f32[8,2048,128]{2,1,0:T(8,128)S(1)}, f32[8,2048,128]{2,1,0:T(8,128)}, u32[]{:S(2)}) copy-start(f32[8,2048,128]{2,1,0:T(8,128)} %gather_fusion) | copy-start | bytes 25165828
  93.7 10.6 %copy-start.8 = (f32[64,16,512]{2,1,0:T(8,128)}, f32[64,16,512]{2,1,0:T(8,128)S(1)}, u32[]{:S(2)}) copy-start(f32[64,16,512]{2,1,0:T(8,128)S(1)} %fusion.75) | copy-start | bytes 6291460
  143.5 7.2 collective-permute-start.2
  144.2 6.5 copy-start.9
  144.2 6.5 copy-start.19
  144.3 6.5 collective-permute-start.3
  162.8 10.7 %copy-start.4 = (f32[64,16,512]{2,1,0:T(8,128)}, f32[64,16,512]{2,1,0:T(8,128)S(1)}, u32[]{:S(2)}) copy-start(f32[64,16,512]{2,1,0:T(8,128)S(1)} %fusion.63) | copy-start | bytes 6291460
  206.4 8.2 %copy-start.5 = (f32[64,16,512]{2,1,0:T(8,128)S(1)}, f32[64,16,512]{2,1,0:T(8,128)}, u32[]{:S(2)}) copy-start(f32[64,16,512]{2,1,0:T(8,128)} %copy-done.4) | copy-start | bytes 6291460
  212.6 7.4 collective-permute-start.4
  213.8 6.2 copy-start.6
  213.8 6.2 copy-start.10
  213.8 6.2 copy-start.17
  213.8 6.2 collective-permute-start.5
  232.3 51.4 %copy-start.2 = (f32[64,16,512]{2,1,0:T(8,128)}, f32[64,16,512]{2,1,0:T(8,128)S(1)}, u32[]{:S(2)}) copy-start(f32[64,16,512]{2,1,0:T(8,128)S(1)} %fusion.50) | copy-start | bytes 6291460
  281.8 7.4 collective-permute-start.6
  283.0 6.2 copy-start.7
  283.0 6.2 copy-start.16
  283.0 6.2 collective-permute-start.7
  352.6 7.3 collective-permute-start.8
  353.7 6.2 copy-start.3
  353.7 6.2 copy-start.18
  353.7 6.1 collective-permute-start.9
  371.9 10.6 %copy-start.11 = (f32[64,16,512]{2,1,0:T(8,128)}, f32[64,16,512]{2,1,0:T(8,128)S(1)}, u32[]{:S(2)}) copy-start(f32[64,16,512]{2,1,0:T(8,128)S(1)} %fusion.24) | copy-start | bytes 6291460
  421.6 7.2 collective-permute-start.10
  422.8 6.1 copy-start.15
  422.8 6.1 collective-permute-start.11
  716.4 52.9 %copy-start.21 = (f32[2,64,1024]{2,1,0:T(8,128)S(1)}, f32[2,64,1024]{2,1,0:T(8,128)}, u32[]{:S(2)}) copy-start(f32[2,64,1024]{2,1,0:T(8,128)} %get-tuple-element.25) | copy-start | bytes 1572868
  728.3 42.3 %copy-start.20 = (f32[2,64,1024]{2,1,0:T(8,128)S(1)}, f32[2,64,1024]{2,1,0:T(8,128)}, u32[]{:S(2)}) copy-start(f32[2,64,1024]{2,1,0:T(8,128)} %get-tuple-element.24) | copy-start | bytes 1572868
  (7 other events, 23.7 us)
Sparse Core Ops, SparseCore 0:
  504.3 129.2 all-reduce.50
where the time goes:
time: 790 us; the launch traced here: 783 us
  matrix products  234 us (30%)
  local copies, waits for them, and re-layouts  203 us (26%)
  waiting for transfers between devices  137 us (17%)
  other arithmetic  123 us (16%)
  blocking collectives  55.2 us (7%)
  between operations  18.9 us (2%)
  starting transfers between devices  11.8 us (1%)
    psum x1, waiting for transfers between devices, local(): gram_matrix = lax.psum(partial_gram, ('band', 'slab'))  128 us
    another operation x15, other arithmetic, local(): factor = jnp.linalg.cholesky(gram_matrix)  79.5 us
    dot_general x6, matrix products, hamiltonian_fn(): jnp.einsum('ajx,anjp->nxp', selector, spread_back, precision=highest)  74.6 us
    dot_general x6, matrix products, hamiltonian_fn(): jnp.einsum('anf,aqf->anq', coupled, atom_tables, precision=highest)  74.1 us
    slice x24, local copies, waits for them, and re-layouts, shifted(): return jnp.concatenate([zeros_part, source[..., :-offset]], axis=-1)  71.5 us
    dot_general x6, matrix products, hamiltonian_fn(): jnp.einsum('anq,aqf->anf', blocks, atom_tables, precision=highest)  56.4 us
    all_to_all x1, blocking collectives, local(): lax.all_to_all(flat_orbitals, 'band', split_axis=1, concat_axis=0, tiled=...  55.2 us
    another operation x4, other arithmetic, local(): return jax.scipy.linalg.solve_triangular(factor, grid_layout, lower=True)  41 us
  transfers between devices with their start and end apart: 13, of which 6 were waited for; matrix products, arithmetic and copies ran while one was open for 11% of the time, Pallas kernels for 0%

commit v1 on v0

v1 whole, which is shorter than its diff:
```python
import functools

import jax
import jax.numpy as jnp
from jax import lax
from jax.experimental import pallas as pl
from jax.experimental.pallas import tpu as pltpu
from jax.sharding import PartitionSpec as P

GZ = 32
ORDER = 6

low_edge = -1.0
highest = lax.Precision.HIGHEST
f32 = jnp.float32
bf16 = jnp.bfloat16


def transverse_matrix(points, width_z):
    r = jnp.arange(points)
    y, z = r // width_z, r % width_z
    dy = jnp.abs(y[:, None] - y[None, :])
    dz = jnp.abs(z[:, None] - z[None, :])
    line = lambda d: jnp.where(d == 0, -30.0, jnp.where(d == 1, 16.0, jnp.where(d == 2, -1.0, 0.0)))
    return (jnp.where(dz == 0, line(dy), 0.0) + jnp.where(dy == 0, line(dz), 0.0)).astype(bf16)


def filter_kernel(
    plane_ref, kind_ref, scal_ref, orb_ref, pot_ref, coef_ref, lap_ref, proj_ref,
    out_ref, ph_ref, pl_ref, buf, split, trans, spread, halo, send_sem, recv_sem,
):
    planes, rows, points = orb_ref.shape
    atoms = coef_ref.shape[0]
    depth = proj_ref.shape[1]
    size = lax.axis_size("slab")
    me = lax.axis_index("slab")
    right, left = lax.rem(me + 1, size), lax.rem(me + size - 1, size)

    barrier = pltpu.get_barrier_semaphore()
    for neighbour in (left, right):
        pl.semaphore_signal(barrier, inc=1, device_id={"slab": neighbour}, device_id_type=pl.DeviceIdType.MESH)
    pl.semaphore_wait(barrier, 2)

    buf[0] = orb_ref[...]
    buf[1] = jnp.zeros((planes, rows, points), f32)
    for a in range(atoms):
        spread[a, 0] = jnp.zeros((rows, points), f32)
        spread[a, depth + 1] = jnp.zeros((rows, points), f32)
    for k in range(proj_ref.shape[0]):
        for j in range(depth):
            table = proj_ref[k, j]
            high = table.astype(bf16)
            ph_ref[k, j] = high
            pl_ref[k, j] = (table - high.astype(f32)).astype(bf16)
    centre = scal_ref[2 * ORDER]

    def step(s, carry):
        cur = lax.rem(s, 2)
        nxt = 1 - cur
        scale = scal_ref[2 * s]
        back = scal_ref[2 * s + 1]
        copies = []
        for side, first, target in ((0, planes - 2, right), (1, 0, left)):
            copy = pltpu.make_async_remote_copy(
                src_ref=buf.at[cur, pl.ds(first, 2)],
                dst_ref=halo.at[s, side],
                send_sem=send_sem.at[side],
                recv_sem=recv_sem.at[s, side],
                device_id={"slab": target},
                device_id_type=pl.DeviceIdType.MESH,
            )
            copy.start()
            copies.append(copy)

        group = 4 if planes % 4 == 0 else 1

        def lap_group(g, c):
            x0 = g * group
            f = buf[cur, pl.ds(x0, group)]
            hi = f.astype(bf16)
            lo = (f - hi.astype(f32)).astype(bf16)
            both = jnp.concatenate([hi, lo], axis=1)
            split[pl.ds(x0, group)] = both
            r = jnp.dot(both.reshape(group * 2 * rows, points), lap_ref[...], preferred_element_type=f32)
            r = r.reshape(group, 2 * rows, points)
            trans[pl.ds(x0, group)] = r[:, :rows] + r[:, rows:]
            return c

        lax.fori_loop(0, planes // group, lap_group, 0)

        def atom(a, c):
            p = plane_ref[a]
            k = kind_ref[a]
            coupled = jnp.zeros((rows, ph_ref.shape[3]), f32)
            for j in range(depth):
                both = split[p + j]
                r = jnp.dot(both, ph_ref[k, j], preferred_element_type=f32)
                e = jnp.dot(both[:rows], pl_ref[k, j], preferred_element_type=f32)
                coupled = coupled + (r[:rows] + (r[rows:] + e))
            coupled = coupled * coef_ref[a]
            hi = coupled.astype(bf16)
            lo = (coupled - hi.astype(f32)).astype(bf16)
            both = jnp.concatenate([hi, lo], axis=0)
            nt = (((1,), (1,)), ((), ()))
            for j in range(depth):
                r = lax.dot_general(both, ph_ref[k, j], nt, preferred_element_type=f32)
                e = lax.dot_general(hi, pl_ref[k, j], nt, preferred_element_type=f32)
                spread[a, j + 1] = r[:rows] + (r[rows:] + e)
            return c

        lax.fori_loop(0, atoms, atom, 0)

        piece = 16 if rows % 16 == 0 else 8

        def plane(x, sources):
            slots = [jnp.clip(x - plane_ref[a], -1, depth) + 1 for a in range(atoms)]
            for r0 in range(0, rows, piece):
                rs = pl.ds(r0, piece)
                f = buf[cur, x, rs]
                m2, m1, p1, p2 = [ref[index + (rs,)] for ref, index in sources]
                total = trans[x, rs] * (-0.5 / 12.0) + (pot_ref[x] + (1.25 - centre)) * f
                total = total + (m1 + p1) * (-2.0 / 3.0) + (m2 + p2) * (1.0 / 24.0)
                for a in range(atoms):
                    total = total + spread[a, slots[a], rs]
                buf[nxt, x, rs] = scale * total - back * buf[nxt, x, rs]

        def interior(x, c):
            plane(x, [(buf, (cur, x + d)) for d in (-2, -1, 1, 2)])
            return c

        lax.fori_loop(2, planes - 2, interior, 0)
        for copy in copies:
            copy.wait()

        def source(x):
            if x < 0:
                return halo, (s, 0, x + 2)
            if x >= planes:
                return halo, (s, 1, x - planes)
            return buf, (cur, x)

        for x in (0, 1, planes - 2, planes - 1):
            plane(x, [source(x + d) for d in (-2, -1, 1, 2)])
        return carry

    lax.fori_loop(0, ORDER, step, 0)
    width = out_ref.shape[2]
    unit = min(width, points)
    for start in range(0, planes * points, unit):
        x, at = start // points, start % points
        chunk, lane = start // width, start % width
        out_ref[chunk, :, lane : lane + unit] = buf[ORDER % 2, x, :, at : at + unit]


def filter_call(plane, kind, scal, orb, pot, coef, lap, tables, chunks):
    planes, rows, points = orb.shape
    atoms = coef.shape[0]
    depth = tables.shape[1]
    smem = pl.BlockSpec(memory_space=pltpu.SMEM)
    vmem = pl.BlockSpec(memory_space=pltpu.VMEM)
    return pl.pallas_call(
        filter_kernel,
        out_shape=jax.ShapeDtypeStruct((chunks, rows, planes * points // chunks), f32),
        in_specs=[smem] * 3 + [vmem] * 5,
        out_specs=vmem,
        scratch_shapes=[
            pltpu.VMEM(tables.shape, bf16),
            pltpu.VMEM(tables.shape, bf16),
            pltpu.VMEM((2, planes, rows, points), f32),
            pltpu.VMEM((planes, 2 * rows, points), bf16),
            pltpu.VMEM((planes, rows, points), f32),
            pltpu.VMEM((atoms, depth + 2, rows, points), f32),
            pltpu.VMEM((ORDER, 2, 2, rows, points), f32),
            pltpu.SemaphoreType.DMA((2,)),
            pltpu.SemaphoreType.DMA((ORDER, 2)),
        ],
        compiler_params=pltpu.CompilerParams(
            collective_id=0, has_side_effects=True, vmem_limit_bytes=56 * 1024 * 1024
        ),
        name="cheb_filter",
    )(plane, kind, scal, orb, pot, coef, lap, tables)


def factor_kernel(nb, g_ref, w_ref, a_ref, d_ref):
    n = g_ref.shape[0]
    a_ref[...] = g_ref[...]
    w_ref[...] = jnp.zeros((n, n), f32)
    rows = lax.broadcasted_iota(jnp.int32, (nb, nb), 0)
    cols = lax.broadcasted_iota(jnp.int32, (nb, nb), 1)
    row_ids = lax.broadcasted_iota(jnp.int32, (nb, 1), 0)
    lane_ids = lax.broadcasted_iota(jnp.int32, (1, nb), 1)
    nt = (((1,), (1,)), ((), ()))
    for b in range(n // nb):
        lo, hi = b * nb, (b + 1) * nb
        d_ref[:, :nb] = a_ref[lo:hi, lo:hi]
        d_ref[:, nb:] = (rows == cols).astype(f32)

        def eliminate(k, c):
            row = d_ref[pl.ds(k, 1), :]
            pivot = jnp.sum(jnp.where(lane_ids == k, row[:, :nb], 0.0), axis=1, keepdims=True)
            column = jnp.sum(jnp.where(cols == k, d_ref[:, :nb], 0.0), axis=1, keepdims=True)
            ratio = jnp.where(row_ids > k, column, 0.0)
            d_ref[...] = d_ref[...] - ratio * (row * (1.0 / pivot))
            return c

        lax.fori_loop(0, nb, eliminate, 0)
        pivots = jnp.sum(jnp.where(rows == cols, d_ref[:, :nb], 0.0), axis=1, keepdims=True)
        inverse = d_ref[:, nb:] / jnp.sqrt(pivots)
        w_ref[lo:hi, lo:hi] = inverse
        if lo > 0:
            mixed = jnp.dot(a_ref[lo:hi, :lo], w_ref[:lo, :lo], precision=highest, preferred_element_type=f32)
            w_ref[lo:hi, :lo] = -jnp.dot(inverse, mixed, precision=highest, preferred_element_type=f32)
        if hi < n:
            panel = lax.dot_general(a_ref[hi:, lo:hi], inverse, nt, precision=highest, preferred_element_type=f32)
            a_ref[hi:, lo:hi] = panel
            a_ref[hi:, hi:] = a_ref[hi:, hi:] - lax.dot_general(
                panel, panel, nt, precision=highest, preferred_element_type=f32
            )


def inverse_factor(gram):
    n = gram.shape[0]
    nb = 128 if n % 128 == 0 else n
    vmem = pl.BlockSpec(memory_space=pltpu.VMEM)
    return pl.pallas_call(
        functools.partial(factor_kernel, nb),
        out_shape=jax.ShapeDtypeStruct((n, n), f32),
        in_specs=[vmem],
        out_specs=vmem,
        scratch_shapes=[pltpu.VMEM((n, n), f32), pltpu.VMEM((nb, 2 * nb), f32)],
        compiler_params=pltpu.CompilerParams(vmem_limit_bytes=32 * 1024 * 1024),
        name="factor_inverse",
    )(gram)


def reduce_axis(value, axis):
    size = lax.axis_size(axis)
    pieces = value.reshape((size, value.shape[0] // size) + value.shape[1:])
    pieces = lax.all_to_all(pieces, axis, split_axis=0, concat_axis=0, tiled=True)
    return jnp.sum(pieces, axis=0)


def gather_axis(value, axis):
    size = lax.axis_size(axis)
    pieces = jnp.broadcast_to(value[None], (size,) + value.shape)
    pieces = lax.all_to_all(pieces, axis, split_axis=0, concat_axis=0, tiled=True)
    return pieces.reshape((size * value.shape[0],) + value.shape[1:])


def local(
    orbitals, potential, projectors, atom_kind, atom_plane, atom_coef, filter_cut, filter_top
):
    band_count, planes, points = orbitals.shape
    kind_count, block_pts, func_count = projectors.shape
    atom_count = atom_kind.shape[0]
    depth = block_pts // points
    bands = lax.axis_size("band")
    local_plane = (atom_plane - lax.axis_index("slab") * planes).astype(jnp.int32)

    cut_value = filter_cut[0]
    top_value = filter_top[0]
    half_width = (top_value - cut_value) / 2.0
    centre = (top_value + cut_value) / 2.0
    sigma_now = half_width / (low_edge - centre)
    tau_value = 2.0 / sigma_now
    scal = [sigma_now / half_width, jnp.zeros((), f32)]
    for _ in range(ORDER - 1):
        sigma_next = 1.0 / (tau_value - sigma_now)
        scal += [2.0 * sigma_next / half_width, sigma_now * sigma_next]
        sigma_now = sigma_next
    scal = jnp.stack(scal + [centre])

    tables = projectors.reshape(kind_count, depth, points, func_count)
    filtered = filter_call(
        local_plane, atom_kind, scal,
        jnp.transpose(orbitals, (1, 0, 2)), potential.reshape(planes, 1, points),
        atom_coef.reshape(atom_count, 1, func_count), transverse_matrix(points, GZ), tables, bands,
    )
    grid_layout = lax.all_to_all(filtered, "band", split_axis=0, concat_axis=0, tiled=True)
    grid_layout = grid_layout.reshape(bands * band_count, planes * points // bands)
    point_total = grid_layout.shape[1] * lax.axis_size(("band", "slab"))
    gram = jnp.dot(grid_layout, grid_layout.T, precision=highest) / point_total
    gram = reduce_axis(reduce_axis(gram, "slab"), "band")
    gram = gather_axis(gather_axis(gram, "band"), "slab")
    return jnp.dot(inverse_factor(gram), grid_layout, precision=lax.Precision.HIGH)


def solution(mesh):
    in_specs = (
        P("band", "slab", None),
        P("slab", None),
        P(),
        P("slab"),
        P("slab"),
        P("slab", None),
        P(),
        P(),
    )
    out_specs = P(None, ("slab", "band"))
    return jax.shard_map(local, mesh=mesh, in_specs=in_specs, out_specs=out_specs, check_vma=False)
```

time: 790 us -> 255 us (0.32)
  matrix products: 234 us -> 6.7 us
  local copies, waits for them, and re-layouts: 203 us -> 6.33 us
  waiting for transfers between devices: 137 us -> 0 us
  Pallas kernels: 0 us -> 125 us
  other arithmetic: 123 us -> 2.28 us
  blocking collectives: 55.2 us -> 112 us
  between operations: 18.9 us -> 1.9 us
  starting transfers between devices: 11.8 us -> 0 us
    dot_general x25 -> x2, matrix products: 226 us -> 6.7 us  [the longest x1 3.52 us: local(): gram = jnp.dot(grid_layout, grid_layout.T, precision=highest) / point_total]
    psum x1 -> x0, waiting for transfers between devices: 128 us -> none  [local(): gram_matrix = lax.psum(partial_gram, ('band', 'slab'))]
    pallas_call x0 -> x2, Pallas kernels: none -> 125 us  [the longest x1 67.5 us: filter_call(): pl.pallas_call(filter_kernel, out_shape=jax.ShapeDtypeStruct((chunks, row...]
    another operation x19 -> x0, other arithmetic: 121 us -> none  [the longest x15 79.5 us: local(): factor = jnp.linalg.cholesky(gram_matrix)]
    slice x30 -> x0, local copies, waits for them, and re-layouts: 74.5 us -> none  [the longest x24 71.5 us: shifted(): return jnp.concatenate([zeros_part, source[..., :-offset]], axis=-1)]
    reshape x12 -> x1, local copies, waits for them, and re-layouts: 73.2 us -> 1.38 us  [local(): potential.reshape(planes, 1, points)]
    all_to_all x1 -> x5, blocking collectives: 55.2 us -> 112 us  [the longest x1 54.8 us: local(): lax.all_to_all(filtered, 'band', split_axis=0, concat_axis=0, tiled=True)]
    transpose x6 -> x0, local copies, waits for them, and re-layouts: 30.7 us -> none  [hamiltonian_fn(): blocks = jnp.einsum('ajx,nxp->anjp', selector, source, precision=highest)]
  transfers between devices with their start and end apart: 13 -> 0, of which waited for: 6 -> 0; matrix products, arithmetic and copies ran while one was open for 11% -> 0% of each run, Pallas kernels for 0% -> 0%
where the time goes in v1:
time: 255 us; the launch traced here: 254 us
  Pallas kernels  125 us (49%)
  blocking collectives  112 us (44%)
  matrix products  6.7 us (3%)
  local copies, waits for them, and re-layouts  6.33 us (2%)
    pallas_call x1, Pallas kernels, filter_call(): pl.pallas_call(filter_kernel, out_shape=jax.ShapeDtypeStruct((chunks, row...  67.5 us
    pallas_call x1, Pallas kernels, inverse_factor(): pl.pallas_call(functools.partial(factor_kernel, nb), out_shape=jax.ShapeD...  57.3 us
    all_to_all x1, blocking collectives, local(): lax.all_to_all(filtered, 'band', split_axis=0, concat_axis=0, tiled=True)  54.8 us
    all_to_all x2, blocking collectives, reduce_axis(): lax.all_to_all(pieces, axis, split_axis=0, concat_axis=0, tiled=True)  28.8 us
    all_to_all x2, blocking collectives, gather_axis(): lax.all_to_all(pieces, axis, split_axis=0, concat_axis=0, tiled=True)  28.8 us

profile of v1, /device:TPU:0, one launch (start us, length us, event | category | flops | bytes accessed | tf_op | source)
XLA Modules:
  0.0 254.5 jit_solution(6864140630988571948)
XLA Ops:
  1.9 1.4 reshape.76.pot_ref
  3.2 0.0 copy-start
  3.2 4.1 %copy.12 = f32[64,16,512]{2,0,1:T(8,128)} copy(f32[64,16,512]{2,1,0:T(8,128)} %param.8) | data formatting | bytes 4194304 | tf_op args[0]
  7.4 0.0 copy-done
  7.4 0.5 broadcast_subtract_fusion.plane_ref
  7.9 1.7 add_convert_fusion.lap_ref
  9.5 0.7 stack.48.scal_ref
  10.2 67.5 %cheb_filter.1 = f32[8,64,1024]{2,1,0:T(8,128)} custom-call(s32[8]{0:T(128)} %broadcast_subtract_fusion.plane_ref, s32[8]{0:T(128)} %kind_ref.1, f32[13]{0:T(128)} %stack.48.scal_ref, f32[16,64,512]{2,1,0:T(8,128)} %bitcast.30, f32[16,1,512]{2,1,0:T(1,128)} %reshape.76.pot_ref, f32[8,1,128]{2,1,0:T(1,128)} %bitcast.35, ...), custom_call_target="tpu_custom_call" | custom-call | tf_op jit(solution)/shard_map/cheb_filter/pallas_call | solution.py:161
  77.7 54.8 %all_to_all.25 = f32[8,64,1024]{2,1,0:T(8,128)S(1)} all-to-all(f32[8,64,1024]{2,1,0:T(8,128)} %cheb_filter.1), channel_id=1, replica_groups=mesh['band'=8,'slab'=4] {'band'}, dimensions={0} | all-to-all | bytes 4194304 | tf_op jit(solution)/shard_map/all_to_all | solution.py:279
  132.6 3.5 %convolution_multiply_fusion = f32[512,512]{1,0:T(8,128)S(1)} fusion(f32[512,1024]{1,0:T(8,128)S(1)} %bitcast.28), kind=kOutput, calls=%fused_computation.1 | convolution fusion | flops 3221487616 | bytes 3145728 | tf_op jit(solution)/shard_map/dot_general | solution.py:282
  136.1 16.9 %all_to_all.26 = f32[4,128,512]{2,1,0:T(8,128)S(1)} all-to-all(f32[4,128,512]{2,1,0:T(8,128)S(1)} %bitcast.31), channel_id=1, replica_groups=mesh['band'=8,'slab'=4] {'slab'}, dimensions={0} | all-to-all | bytes 2097152 | tf_op jit(solution)/shard_map/all_to_all | solution.py:239
  153.0 0.1 reduce_sum.18
  153.1 12.0 %all_to_all.27 = f32[8,16,512]{2,1,0:T(8,128)S(1)} all-to-all(f32[8,16,512]{2,1,0:T(8,128)S(1)} %bitcast.33), channel_id=1, replica_groups=mesh['band'=8,'slab'=4] {'band'}, dimensions={0} | all-to-all | bytes 524288 | tf_op jit(solution)/shard_map/all_to_all | solution.py:239
  165.1 11.9 %all_to_all.28 = f32[8,16,512]{2,1,0:T(8,128)S(1)} all-to-all(f32[8,16,512]{2,1,0:T(8,128)S(1)} %broadcast_in_dim.43), channel_id=1, replica_groups=mesh['band'=8,'slab'=4] {'band'}, dimensions={0} | all-to-all | bytes 524288 | tf_op jit(solution)/shard_map/all_to_all | solution.py:246
  177.0 0.1 broadcast_in_dim.45
  177.1 16.9 %all_to_all.29 = f32[4,128,512]{2,1,0:T(8,128)S(1)} all-to-all(f32[4,128,512]{2,1,0:T(8,128)S(1)} %broadcast_in_dim.45), channel_id=1, replica_groups=mesh['band'=8,'slab'=4] {'slab'}, dimensions={0} | all-to-all | bytes 2097152 | tf_op jit(solution)/shard_map/all_to_all | solution.py:246
  194.0 57.3 %factor_inverse.1 = f32[512,512]{1,0:T(8,128)S(1)} custom-call(f32[512,512]{1,0:T(8,128)S(1)} %bitcast.27), custom_call_target="tpu_custom_call" | custom-call | tf_op jit(solution)/shard_map/factor_inverse/pallas_call | solution.py:225
  251.3 3.2 %fusion.11 = f32[512,1024]{1,0:T(8,128)} fusion(f32[512,512]{1,0:T(8,128)S(1)} %factor_inverse.1, f32[512,1024]{1,0:T(8,128)S(1)} %bitcast.29), kind=kOutput, calls=%fused_computation.22 | convolution fusion | flops 1610612736 | bytes 5242880 | tf_op jit(solution)/shard_map/dot_general | solution.py:285
  (3 shorter events, 0.0 us)
Async XLA Ops:
  3.2 4.1 %copy-start = (s32[8]{0:T(128)S(1)}, s32[8]{0:T(128)}, u32[]{:S(2)}) copy-start(s32[8]{0:T(128)} %param.12) | copy-start | bytes 100

commit v2 on v1

--- a/solution.py
+++ b/solution.py
@@ -182,8 +182,13 @@
 
 
 def factor_kernel(nb, g_ref, w_ref, a_ref, d_ref):
-    n = g_ref.shape[0]
-    a_ref[...] = g_ref[...]
+    n = w_ref.shape[0]
+    a_ref[...] = jnp.zeros((n, n), f32)
+    at = 0
+    for i in range(n // nb):
+        for j in range(i + 1):
+            a_ref[i * nb : (i + 1) * nb, j * nb : (j + 1) * nb] = g_ref[at : at + nb]
+            at += nb
     w_ref[...] = jnp.zeros((n, n), f32)
     rows = lax.broadcasted_iota(jnp.int32, (nb, nb), 0)
     cols = lax.broadcasted_iota(jnp.int32, (nb, nb), 1)
@@ -218,9 +223,8 @@
             )
 
 
-def inverse_factor(gram):
-    n = gram.shape[0]
-    nb = 128 if n % 128 == 0 else n
+def inverse_factor(blocks, n):
+    nb = block_size(n)
     vmem = pl.BlockSpec(memory_space=pltpu.VMEM)
     return pl.pallas_call(
         functools.partial(factor_kernel, nb),
@@ -230,21 +234,113 @@
         scratch_shapes=[pltpu.VMEM((n, n), f32), pltpu.VMEM((nb, 2 * nb), f32)],
         compiler_params=pltpu.CompilerParams(vmem_limit_bytes=32 * 1024 * 1024),
         name="factor_inverse",
+    )(blocks)
+
+
+def reduce_kernel(nb, g_ref, out_ref, pack, first, part, second, full, sends, recvs_a, recvs_b, recvs_c, recvs_d):
+    n = g_ref.shape[0]
+    total = pack.shape[0]
+    slabs, bands = lax.axis_size("slab"), lax.axis_size("band")
+    my_slab, my_band = lax.axis_index("slab"), lax.axis_index("band")
+    deep, thin = total // slabs, total // slabs // bands
+    at = 0
+    for i in range(n // nb):
+        for j in range(i + 1):
+            pack[at : at + nb] = g_ref[i * nb : (i + 1) * nb, j * nb : (j + 1) * nb]
+            at += nb
+    if at < total:
+        pack[at:] = jnp.zeros((total - at, nb), f32)
+
+    def peer(me, size, d):
+        return lax.rem(me + d, size)
+
+    barrier = pltpu.get_barrier_semaphore()
+    for axis, me, size in (("slab", my_slab, slabs), ("band", my_band, bands)):
+        for d in range(1, size):
+            pl.semaphore_signal(
+                barrier, inc=1, device_id={axis: peer(me, size, d)}, device_id_type=pl.DeviceIdType.MESH
+            )
+    pl.semaphore_wait(barrier, slabs + bands - 2)
+
+    def exchange(axis, me, size, source, target, recvs):
+        copies = []
+        for d in range(1, size):
+            other = peer(me, size, d)
+            copies.append(
+                pltpu.make_async_remote_copy(
+                    src_ref=source(other),
+                    dst_ref=target(d),
+                    send_sem=sends.at[d - 1],
+                    recv_sem=recvs.at[d - 1],
+                    device_id={axis: other},
+                    device_id_type=pl.DeviceIdType.MESH,
+                )
+            )
+        for copy in copies:
+            copy.start()
+        for copy in copies:
+            copy.wait()
+
+    def span(start, length):
+        return pl.ds(pl.multiple_of(start, 8), length)
+
+    exchange(
+        "slab", my_slab, slabs, lambda t: pack.at[span(t * deep, deep)], lambda d: first.at[d - 1], recvs_a
+    )
+    value = pack[span(my_slab * deep, deep)]
+    for d in range(1, slabs):
+        value = value + first[d - 1]
+    part[...] = value
+    exchange(
+        "band", my_band, bands, lambda t: part.at[span(t * thin, thin)], lambda d: second.at[d - 1], recvs_b
+    )
+    value = part[span(my_band * thin, thin)]
+    for d in range(1, bands):
+        value = value + second[d - 1]
+    mine = span(my_slab * deep + my_band * thin, thin)
+    full[mine] = value
+    exchange("band", my_band, bands, lambda t: full.at[mine], lambda d: full.at[mine], recvs_c)
+    mine_deep = span(my_slab * deep, deep)
+    exchange("slab", my_slab, slabs, lambda t: full.at[mine_deep], lambda d: full.at[mine_deep], recvs_d)
+    out_ref[...] = full[...]
+
+
+def block_size(n):
+    return 128 if n % 128 == 0 else n
+
+
+def reduced_blocks(gram):
+    n = gram.shape[0]
+    nb = block_size(n)
+    slabs, bands = lax.axis_size("slab"), lax.axis_size("band")
+    count = n // nb
+    used = count * (count + 1) // 2 * nb
+    unit = 8 * slabs * bands
+    total = (used + unit - 1) // unit * unit
+    vmem = pl.BlockSpec(memory_space=pltpu.VMEM)
+    dma = pltpu.SemaphoreType.DMA
+    return pl.pallas_call(
+        functools.partial(reduce_kernel, nb),
+        out_shape=jax.ShapeDtypeStruct((total, nb), f32),
+        in_specs=[vmem],
+        out_specs=vmem,
+        scratch_shapes=[
+            pltpu.VMEM((total, nb), f32),
+            pltpu.VMEM((slabs - 1, total // slabs, nb), f32),
+            pltpu.VMEM((total // slabs, nb), f32),
+            pltpu.VMEM((bands - 1, total // slabs // bands, nb), f32),
+            pltpu.VMEM((total, nb), f32),
+            dma((max(slabs, bands) - 1,)),
+            dma((slabs - 1,)),
+            dma((bands - 1,)),
+            dma((bands - 1,)),
+            dma((slabs - 1,)),
+        ],
+        compiler_params=pltpu.CompilerParams(
+            collective_id=1, has_side_effects=True, vmem_limit_bytes=32 * 1024 * 1024
+        ),
+        name="gram_sum",
     )(gram)
-
-
-def reduce_axis(value, axis):
-    size = lax.axis_size(axis)
-    pieces = value.reshape((size, value.shape[0] // size) + value.shape[1:])
-    pieces = lax.all_to_all(pieces, axis, split_axis=0, concat_axis=0, tiled=True)
-    return jnp.sum(pieces, axis=0)
-
-
-def gather_axis(value, axis):
-    size = lax.axis_size(axis)
-    pieces = jnp.broadcast_to(value[None], (size,) + value.shape)
-    pieces = lax.all_to_all(pieces, axis, split_axis=0, concat_axis=0, tiled=True)
-    return pieces.reshape((size * value.shape[0],) + value.shape[1:])
 
 
 def local(
@@ -280,9 +376,8 @@
     grid_layout = grid_layout.reshape(bands * band_count, planes * points // bands)
     point_total = grid_layout.shape[1] * lax.axis_size(("band", "slab"))
     gram = jnp.dot(grid_layout, grid_layout.T, precision=highest) / point_total
-    gram = reduce_axis(reduce_axis(gram, "slab"), "band")
-    gram = gather_axis(gather_axis(gram, "band"), "slab")
-    return jnp.dot(inverse_factor(gram), grid_layout, precision=lax.Precision.HIGH)
+    factor_inverse = inverse_factor(reduced_blocks(gram), gram.shape[0])
+    return jnp.dot(factor_inverse, grid_layout, precision=lax.Precision.HIGH)
 
 
 def solution(mesh):

time: 255 us -> 224 us (0.88)
  blocking collectives: 112 us -> 54.8 us
  Pallas kernels: 125 us -> 152 us
    all_to_all x4 -> x0, blocking collectives: 57.6 us -> none  [the longest x2 28.8 us: reduce_axis(): lax.all_to_all(pieces, axis, split_axis=0, concat_axis=0, tiled=True)]
    pallas_call x0 -> x1, Pallas kernels: none -> 27.3 us  [reduced_blocks(): pl.pallas_call(functools.partial(reduce_kernel, nb), out_shape=jax.ShapeD...]
where the time goes in v2:
time: 224 us
  Pallas kernels  152 us (68%)
  blocking collectives  54.8 us (24%)
  matrix products  6.69 us (3%)
  local copies, waits for them, and re-layouts  6.21 us (3%)
  other arithmetic  2.25 us (1%)
    pallas_call x1, Pallas kernels, filter_call(): pl.pallas_call(filter_kernel, out_shape=jax.ShapeDtypeStruct((chunks, row...  67.5 us
    pallas_call x1, Pallas kernels, inverse_factor(): pl.pallas_call(functools.partial(factor_kernel, nb), out_shape=jax.ShapeD...  56.9 us
    all_to_all x1, blocking collectives, local(): lax.all_to_all(filtered, 'band', split_axis=0, concat_axis=0, tiled=True)  54.8 us
    pallas_call x1, Pallas kernels, reduced_blocks(): pl.pallas_call(functools.partial(reduce_kernel, nb), out_shape=jax.ShapeD...  27.3 us

profile of v2, /device:TPU:0, one launch (start us, length us, event | category | flops | bytes accessed | tf_op | source)
XLA Modules:
  0.0 223.6 jit_solution(6128543066085430183)
XLA Ops:
  1.9 1.4 reshape.65.pot_ref
  3.2 0.0 copy-start
  3.2 4.1 %copy.11 = f32[64,16,512]{2,0,1:T(8,128)} copy(f32[64,16,512]{2,1,0:T(8,128)} %param.8) | data formatting | bytes 4194304 | tf_op args[0]
  7.4 0.0 copy-done
  7.4 0.6 broadcast_subtract_fusion.plane_ref
  8.0 1.7 add_convert_fusion.lap_ref
  9.6 0.7 stack.48.scal_ref
  10.3 67.5 %cheb_filter.1 = f32[8,64,1024]{2,1,0:T(8,128)} custom-call(s32[8]{0:T(128)} %broadcast_subtract_fusion.plane_ref, s32[8]{0:T(128)} %kind_ref.1, f32[13]{0:T(128)} %stack.48.scal_ref, f32[16,64,512]{2,1,0:T(8,128)} %bitcast.25, f32[16,1,512]{2,1,0:T(1,128)} %reshape.65.pot_ref, f32[8,1,128]{2,1,0:T(1,128)} %bitcast.27, ...), custom_call_target="tpu_custom_call" | custom-call | tf_op jit(solution)/shard_map/cheb_filter/pallas_call | solution.py:161
  77.8 54.8 %all_to_all.5 = f32[8,64,1024]{2,1,0:T(8,128)S(1)} all-to-all(f32[8,64,1024]{2,1,0:T(8,128)} %cheb_filter.1), channel_id=1, replica_groups=mesh['band'=8,'slab'=4] {'band'}, dimensions={0} | all-to-all | bytes 4194304 | tf_op jit(solution)/shard_map/all_to_all | solution.py:375
  132.7 3.5 %convolution_multiply_fusion.g_ref = f32[512,512]{1,0:T(8,128)S(1)} fusion(f32[512,1024]{1,0:T(8,128)S(1)} %bitcast.23), kind=kOutput, calls=%fused_computation.1 | convolution fusion | flops 3221487616 | bytes 3145728 | tf_op jit(solution)/shard_map/dot_general | solution.py:378
  136.2 27.3 %gram_sum.1.g_ref = f32[1280,128]{1,0:T(8,128)S(1)} custom-call(f32[512,512]{1,0:T(8,128)S(1)} %convolution_multiply_fusion.g_ref), custom_call_target="tpu_custom_call" | custom-call | tf_op jit(solution)/shard_map/gram_sum/pallas_call | solution.py:322
  163.5 56.9 %factor_inverse.1 = f32[512,512]{1,0:T(8,128)S(1)} custom-call(f32[1280,128]{1,0:T(8,128)S(1)} %gram_sum.1.g_ref), custom_call_target="tpu_custom_call" | custom-call | tf_op jit(solution)/shard_map/factor_inverse/pallas_call | solution.py:229
  220.4 3.2 %fusion.11 = f32[512,1024]{1,0:T(8,128)} fusion(f32[512,512]{1,0:T(8,128)S(1)} %factor_inverse.1, f32[512,1024]{1,0:T(8,128)S(1)} %bitcast.24), kind=kOutput, calls=%fused_computation.22 | convolution fusion | flops 1610612736 | bytes 5242880 | tf_op jit(solution)/shard_map/dot_general | solution.py:380
  (1 shorter events, 0.0 us)
Async XLA Ops:
  3.2 4.1 %copy-start = (s32[8]{0:T(128)S(1)}, s32[8]{0:T(128)}, u32[]{:S(2)}) copy-start(s32[8]{0:T(128)} %param.12) | copy-start | bytes 100

commit v3 on v2

--- a/solution.py
+++ b/solution.py
@@ -200,15 +200,30 @@
         d_ref[:, :nb] = a_ref[lo:hi, lo:hi]
         d_ref[:, nb:] = (rows == cols).astype(f32)
 
-        def eliminate(k, c):
-            row = d_ref[pl.ds(k, 1), :]
-            pivot = jnp.sum(jnp.where(lane_ids == k, row[:, :nb], 0.0), axis=1, keepdims=True)
-            column = jnp.sum(jnp.where(cols == k, d_ref[:, :nb], 0.0), axis=1, keepdims=True)
-            ratio = jnp.where(row_ids > k, column, 0.0)
-            d_ref[...] = d_ref[...] - ratio * (row * (1.0 / pivot))
+        def eliminate(t, c):
+            k = 2 * t
+            top = d_ref[pl.ds(k, 1), :]
+            low = d_ref[pl.ds(k + 1, 1), :]
+            block = d_ref[:, :nb]
+
+            def lane(row, at):
+                return jnp.sum(jnp.where(lane_ids == at, row[:, :nb], 0.0), axis=1, keepdims=True)
+
+            def column(at):
+                return jnp.sum(jnp.where(cols == at, block, 0.0), axis=1, keepdims=True)
+
+            p11, p12, p22 = lane(top, k), lane(top, k + 1), lane(low, k + 1)
+            c0, c1 = column(k), column(k + 1)
+            inv1 = 1.0 / p11
+            link = p12 * inv1
+            inv2 = 1.0 / (p22 - p12 * link)
+            low = (low - link * top) * inv2
+            c1 = jnp.where(row_ids > k + 1, c1 - link * c0, 0.0)
+            c0 = jnp.where(row_ids > k, c0, 0.0)
+            d_ref[...] = d_ref[...] - c0 * (top * inv1) - c1 * low
             return c
 
-        lax.fori_loop(0, nb, eliminate, 0)
+        lax.fori_loop(0, nb // 2, eliminate, 0)
         pivots = jnp.sum(jnp.where(rows == cols, d_ref[:, :nb], 0.0), axis=1, keepdims=True)
         inverse = d_ref[:, nb:] / jnp.sqrt(pivots)
         w_ref[lo:hi, lo:hi] = inverse

time: 224 us -> 203 us (0.906)
  Pallas kernels: 152 us -> 130 us
    pallas_call x1, Pallas kernels: 56.9 us -> 35.6 us  [inverse_factor(): pl.pallas_call(functools.partial(factor_kernel, nb), out_shape=jax.ShapeD...]
where the time goes in v3:
time: 203 us; the launch traced here: 202 us
  Pallas kernels  130 us (64%)
  blocking collectives  54.8 us (27%)
  matrix products  6.69 us (3%)
  local copies, waits for them, and re-layouts  6.21 us (3%)
  other arithmetic  2.25 us (1%)
    pallas_call x1, Pallas kernels, filter_call(): pl.pallas_call(filter_kernel, out_shape=jax.ShapeDtypeStruct((chunks, row...  67.5 us
    all_to_all x1, blocking collectives, local(): lax.all_to_all(filtered, 'band', split_axis=0, concat_axis=0, tiled=True)  54.8 us
    pallas_call x1, Pallas kernels, inverse_factor(): pl.pallas_call(functools.partial(factor_kernel, nb), out_shape=jax.ShapeD...  35.6 us
    pallas_call x1, Pallas kernels, reduced_blocks(): pl.pallas_call(functools.partial(reduce_kernel, nb), out_shape=jax.ShapeD...  27.3 us
    unnamed x3, local copies, waits for them, and re-layouts  4.14 us

profile of v3, /device:TPU:0, one launch (start us, length us, event | category | flops | bytes accessed | tf_op | source)
XLA Modules:
  0.0 202.3 jit_solution(9125169677745095523)
XLA Ops:
  1.9 1.4 reshape.65.pot_ref
  3.2 0.0 copy-start
  3.2 4.1 %copy.11 = f32[64,16,512]{2,0,1:T(8,128)} copy(f32[64,16,512]{2,1,0:T(8,128)} %param.8) | data formatting | bytes 4194304 | tf_op args[0]
  7.4 0.0 copy-done
  7.4 0.6 broadcast_subtract_fusion.plane_ref
  8.0 1.7 add_convert_fusion.lap_ref
  9.6 0.7 stack.48.scal_ref
  10.3 67.5 %cheb_filter.1 = f32[8,64,1024]{2,1,0:T(8,128)} custom-call(s32[8]{0:T(128)} %broadcast_subtract_fusion.plane_ref, s32[8]{0:T(128)} %kind_ref.1, f32[13]{0:T(128)} %stack.48.scal_ref, f32[16,64,512]{2,1,0:T(8,128)} %bitcast.25, f32[16,1,512]{2,1,0:T(1,128)} %reshape.65.pot_ref, f32[8,1,128]{2,1,0:T(1,128)} %bitcast.27, ...), custom_call_target="tpu_custom_call" | custom-call | tf_op jit(solution)/shard_map/cheb_filter/pallas_call | solution.py:161
  77.8 54.8 %all_to_all.5 = f32[8,64,1024]{2,1,0:T(8,128)S(1)} all-to-all(f32[8,64,1024]{2,1,0:T(8,128)} %cheb_filter.1), channel_id=1, replica_groups=mesh['band'=8,'slab'=4] {'band'}, dimensions={0} | all-to-all | bytes 4194304 | tf_op jit(solution)/shard_map/all_to_all | solution.py:390
  132.7 3.5 %convolution_multiply_fusion.g_ref = f32[512,512]{1,0:T(8,128)S(1)} fusion(f32[512,1024]{1,0:T(8,128)S(1)} %bitcast.23), kind=kOutput, calls=%fused_computation.1 | convolution fusion | flops 3221487616 | bytes 3145728 | tf_op jit(solution)/shard_map/dot_general | solution.py:393
  136.2 27.3 %gram_sum.1.g_ref = f32[1280,128]{1,0:T(8,128)S(1)} custom-call(f32[512,512]{1,0:T(8,128)S(1)} %convolution_multiply_fusion.g_ref), custom_call_target="tpu_custom_call" | custom-call | tf_op jit(solution)/shard_map/gram_sum/pallas_call | solution.py:337
  163.5 35.6 %factor_inverse.1 = f32[512,512]{1,0:T(8,128)S(1)} custom-call(f32[1280,128]{1,0:T(8,128)S(1)} %gram_sum.1.g_ref), custom_call_target="tpu_custom_call" | custom-call | tf_op jit(solution)/shard_map/factor_inverse/pallas_call | solution.py:244
  199.1 3.2 %fusion.11 = f32[512,1024]{1,0:T(8,128)} fusion(f32[512,512]{1,0:T(8,128)S(1)} %factor_inverse.1, f32[512,1024]{1,0:T(8,128)S(1)} %bitcast.24), kind=kOutput, calls=%fused_computation.22 | convolution fusion | flops 1610612736 | bytes 5242880 | tf_op jit(solution)/shard_map/dot_general | solution.py:395
  (1 shorter events, 0.0 us)
Async XLA Ops:
  3.2 4.1 %copy-start = (s32[8]{0:T(128)S(1)}, s32[8]{0:T(128)}, u32[]{:S(2)}) copy-start(s32[8]{0:T(128)} %param.12) | copy-start | bytes 100
